TPU v7x, 32 devices: a whole 2x2x4 slice. The times are simulated.
32 devices in a mesh: lat: 16 (over z, x, core), lon: 2 (over y).
Axes of the slice: x: 2, y: 2, z: 4, core: 2. Of those that a mesh axis runs over, the one named last changes fastest.
Arguments:
- elevation: float32 [4096, 4096], P('lat', 'lon'), may hold values from -200 to 200
Outputs:
- slope_angle: float32 [4096, 4096], P('lat', 'lon')
- facing: float32 [2, 4096, 4096], P(None, 'lat', 'lon')
- hillshade: float32 [4096, 4096], P('lat', 'lon')
All inputs are finite; a program needn't handle non-finite values.
Results may differ from a plain program's by a relative error of at most 0.0003.
Values sent between devices are 32-bit elements; how exact they have to be, the bound alone decides.
A program may use at most 64 MiB of HBM per device.

v0:
```python
import functools
import math

import jax
import jax.numpy as jnp
from jax import lax
from jax.experimental import pallas as pl
from jax.experimental.pallas import tpu as pltpu
from jax.sharding import PartitionSpec as P

SCALES = 7
HALO = 64
LANES = 128
SUB = 8
RUNS = 2

LIGHT_UP = math.sqrt(0.5)
MESH = pl.DeviceIdType.MESH

ANGLE = (
    1.5707962050889646,
    -0.9999801696091738,
    0.7848538132927688,
    -0.6607586188432167,
    0.5557489578459907,
    -0.42189571811945836,
    0.2501265286961767,
    -0.09607630454800326,
    0.01718536914918157,
)


def row_pad(octave):
    return max(2**octave, SUB)


def near_side(lat):
    return 1 - lax.rem(lat, 2)


def fill_coef(coef_ref, count, first_row, total_rows, total_cols):
    for start in range(0, count, SUB):
        position = first_row + start + lax.broadcasted_iota(jnp.int32, (SUB, LANES), 0)
        spacing = jnp.sin((position.astype(jnp.float32) + 0.5) * (math.pi / total_rows)) * (
            2.0 * total_rows / total_cols
        )
        coef_ref[pl.ds(start, SUB), :] = 1.0 / (8.0 * SCALES * spacing)


class Window:
    def __init__(self, strips, base, count, width, boxes, sums, coef, slope, facing, shade):
        self.strips, self.base, self.count, self.width = strips, base, count, width
        self.boxes, self.sums, self.coef = boxes, sums, coef
        self.slope, self.facing, self.shade = slope, facing, shade
        self.lane = lax.broadcasted_iota(jnp.int32, (SUB, LANES), 1)

    def here(self, starts, row):
        top = pl.multiple_of(self.base + row, SUB)
        return [
            [self.strips[start + k, pl.ds(top, SUB), :] for k in range(self.width + 2)]
            for start in starts
        ]

    def box(self, starts, row, octave, here):
        lag = 2**octave
        top = pl.multiple_of(self.base + row, SUB)
        boxes, shifted = [], []
        for start, z in zip(starts, here):
            pair = []
            for k in range(self.width + 2):
                total = z[k] + self.strips[start + k, pl.ds(top + lag, SUB), :]
                pair.append(total * (1.0 / lag) if octave else total)
            ahead = [pltpu.roll(v, LANES - lag, 1) for v in pair]
            if 2 * lag == LANES:
                plus = [
                    jnp.where(self.lane < lag, ahead[k], ahead[k + 1])
                    for k in range(self.width + 1)
                ]
                boxes += [pair[k + 1] + plus[k + 1] for k in range(self.width)]
                shifted += [pair[k + 1] + plus[k] for k in range(self.width)]
            else:
                behind = [pltpu.roll(v, lag, 1) for v in pair]
                for k in range(1, self.width + 1):
                    plus = jnp.where(self.lane < LANES - lag, ahead[k], ahead[k + 1])
                    minus = jnp.where(self.lane >= lag, behind[k], behind[k - 1])
                    boxes.append(pair[k] + plus)
                    shifted.append(pair[k] + minus)
        return boxes, shifted

    def keep(self, row, octave, boxes, shifted):
        place = pl.ds(pl.multiple_of(row + row_pad(octave), SUB), SUB)
        for k in range(RUNS * self.width):
            self.boxes[octave][0, k, place, :] = boxes[k]
            self.boxes[octave][1, k, place, :] = shifted[k]

    def before(self, starts):
        for distance in range(SUB, HALO + SUB, SUB):
            here = self.here(starts, -distance)
            for octave in range(SCALES):
                if row_pad(octave) >= distance:
                    boxes, shifted = self.box(starts, -distance, octave, here)
                    self.keep(-distance, octave, boxes, shifted)

    def add(self, starts, row):
        here = self.here(starts, row)
        first = second = None
        for octave in range(SCALES):
            boxes, shifted = self.box(starts, row, octave, here)
            self.keep(row, octave, boxes, shifted)
            past = pl.ds(row + row_pad(octave) - 2**octave, SUB)
            u = [boxes[k] - self.boxes[octave][1, k, past, :] for k in range(RUNS * self.width)]
            v = [self.boxes[octave][0, k, past, :] - shifted[k] for k in range(RUNS * self.width)]
            first = u if first is None else [a + b for a, b in zip(first, u)]
            second = v if second is None else [a + b for a, b in zip(second, v)]
        return first, second

    def hold(self, first, second):
        for k in range(RUNS * self.width):
            self.sums[0, k] = first[k]
            self.sums[1, k] = second[k]

    def held(self):
        count = RUNS * self.width
        return [self.sums[0, k] for k in range(count)], [self.sums[1, k] for k in range(count)]

    def finish(self, starts, row, first, second):
        rows = pl.ds(row, SUB)
        coef = self.coef[rows, :]
        for k in range(RUNS * self.width):
            run, within = divmod(k, self.width)
            column = pl.ds(pl.multiple_of((starts[run] + within) * LANES, LANES), LANES)
            grad_east = (first[k] + second[k]) * coef
            grad_north = (second[k] - first[k]) * (1.0 / (8.0 * SCALES))
            squared = grad_east * grad_east + grad_north * grad_north
            inverse = lax.rsqrt(1.0 + squared)
            sine = squared * lax.rsqrt(jnp.maximum(squared, 1e-37)) * inverse
            ratio = jnp.full_like(inverse, ANGLE[-1])
            for term in ANGLE[-2::-1]:
                ratio = ratio * inverse + term
            self.slope[rows, column] = sine * ratio
            self.facing[0, rows, column] = -grad_east * inverse
            self.facing[1, rows, column] = -grad_north * inverse
            tilt = 0.5 * (grad_east - grad_north) + LIGHT_UP
            self.shade[rows, column] = jnp.maximum(tilt * inverse, 0.0)

    def run(self, starts):
        self.before(starts)
        self.hold(*self.add(starts, 0))

        def step(number, carry):
            row = pl.multiple_of(number * SUB, SUB)
            first, second = self.held()
            sums = self.add(starts, row)
            self.finish(starts, pl.multiple_of(row - SUB, SUB), first, second)
            self.hold(*sums)
            return carry

        lax.fori_loop(1, self.count // SUB, step, 0)
        self.finish(starts, self.count - SUB, *self.held())


def run_starts(half, strips):
    quarter = strips // 4
    return (
        jnp.where(half == 0, quarter, 0),
        jnp.where(half == 0, 2 * quarter, 3 * quarter),
    )


def gather(rows, cols, z_ref, strips_ref, slope, facing, shade, *scratch):
    boxes, (sums, coef, load_sem, send_sem, recv_sem, rim_send, rim_recv) = (
        scratch[:SCALES],
        scratch[SCALES:],
    )
    lat, lon = lax.axis_index("lat"), lax.axis_index("lon")
    n_lat, n_lon = lax.axis_size("lat"), lax.axis_size("lon")
    west, east = lax.rem(lon + n_lon - 1, n_lon), lax.rem(lon + 1, n_lon)
    strips = cols // LANES
    near = near_side(lat)
    far = 1 - near
    exists = (lat > 0, lat < n_lat - 1)
    far_exists = jnp.where(far == 0, exists[0], exists[1])
    far_lat = jnp.where(far == 0, lat - 1, lat + 1)
    near_lat = jnp.where(near == 0, lat - 1, lat + 1)

    def edge(side):
        return pl.multiple_of(jnp.where(side == 0, 0, rows - HALO), SUB)

    def halo(side):
        return pl.multiple_of(jnp.where(side == 0, 0, HALO + rows), SUB)

    def loads_of(number):
        start, count = ((edge(far), HALO), (edge(near), HALO), (HALO, rows - 2 * HALO))[number]
        return [
            pltpu.make_async_copy(
                z_ref.at[pl.ds(start, count), pl.ds(strip * LANES, LANES)],
                strips_ref.at[1 + strip, pl.ds(HALO + start, count), :],
                load_sem.at[number, strip],
            )
            for strip in range(strips)
        ]

    for number in range(3):
        for load in loads_of(number):
            load.start()

    barrier = pltpu.get_barrier_semaphore()

    @pl.when(far_exists)
    def _():
        for other in (lon, west, east):
            pl.semaphore_signal(barrier, inc=1, device_id=(far_lat, other), device_id_type=MESH)

    for other in (west, east):
        pl.semaphore_signal(barrier, inc=1, device_id=(lat, other), device_id_type=MESH)
    for other in (lon, west, east):
        pl.semaphore_signal(barrier, inc=1, device_id=(near_lat, other), device_id_type=MESH)

    main = rows - HALO
    base = pl.multiple_of(jnp.where(far == 0, HALO, 0), SUB)
    fill_coef(coef, main, lat * rows + base, rows * n_lat, cols * n_lon)
    pl.semaphore_wait(barrier, 5 + 3 * far_exists.astype(jnp.int32))

    def lat_copy(distant, kind):
        side, other = (far, far_lat) if distant else (near, near_lat)
        source, target, count, other_lon = (
            (1, 1, strips, lon),
            (1, strips + 1, 1, west),
            (strips, 0, 1, east),
        )[kind]
        return pltpu.make_async_remote_copy(
            src_ref=strips_ref.at[pl.ds(source, count), pl.ds(HALO + edge(side), HALO), :],
            dst_ref=strips_ref.at[pl.ds(target, count), pl.ds(halo(1 - side), HALO), :],
            send_sem=send_sem.at[distant, kind],
            recv_sem=recv_sem.at[distant, kind],
            device_id=(other, other_lon),
            device_id_type=MESH,
        )

    def rim_copy(side):
        source, target, other = ((1, strips + 1, west), (strips, 0, east))[side]
        return pltpu.make_async_remote_copy(
            src_ref=strips_ref.at[source, pl.ds(HALO, rows), :],
            dst_ref=strips_ref.at[target, pl.ds(HALO, rows), :],
            send_sem=rim_send.at[side],
            recv_sem=rim_recv.at[side],
            device_id=(lat, other),
            device_id_type=MESH,
        )

    def lat_arrived(distant, kind):
        side = far if distant else near
        target, count = ((1, strips), (strips + 1, 1), (0, 1))[kind]
        here = strips_ref.at[pl.ds(target, count), pl.ds(halo(side), HALO), :]
        pltpu.make_async_remote_copy(
            src_ref=here,
            dst_ref=here,
            send_sem=send_sem.at[distant, kind],
            recv_sem=recv_sem.at[distant, kind],
            device_id=(lat, east),
            device_id_type=MESH,
        ).wait_recv()

    for load in loads_of(0):
        load.wait()

    @pl.when(far_exists)
    def _():
        lat_copy(1, 0).start()

    for load in loads_of(1):
        load.wait()
    lat_copy(0, 0).start()
    for load in loads_of(2):
        load.wait()
    for side in range(2):
        rim_copy(side).start()
    for kind in (1, 2):
        lat_copy(0, kind).start()

    @pl.when(far_exists)
    def _():
        for kind in (1, 2):
            lat_copy(1, kind).start()

    window = Window(
        strips_ref, HALO + base, main, strips // 4, boxes, sums, coef, slope, facing, shade
    )
    lat_arrived(0, 0)

    def half(number, carry):
        @pl.when(number == 1)
        def _():
            for side in range(2):
                rim_copy(side).wait_recv()
            for kind in (1, 2):
                lat_arrived(0, kind)

        window.run(run_starts(number, strips))
        return carry

    lax.fori_loop(0, 2, half, 0)

    for pole in range(2):

        @pl.when(jnp.logical_and(jnp.logical_not(far_exists), far == pole))
        def _():
            first = HALO if pole == 0 else HALO + rows - SUB
            pick = 0 if pole == 0 else SUB - 1
            fill = 0 if pole == 0 else HALO + rows

            def repeat(strip, carry):
                row = strips_ref[strip, pl.ds(first, SUB), :][pick : pick + 1]
                block = jnp.broadcast_to(row, (SUB, LANES))
                for k in range(HALO // SUB):
                    strips_ref[strip, pl.ds(fill + k * SUB, SUB), :] = block
                return carry

            lax.fori_loop(0, strips + 2, repeat, 0)

    for side in range(2):
        rim_copy(side).wait_send()
    for kind in range(3):
        lat_copy(0, kind).wait_send()

    @pl.when(far_exists)
    def _():
        for kind in range(3):
            lat_arrived(1, kind)
            lat_copy(1, kind).wait_send()


def shade_far(rows, cols, *refs):
    strips_ref, slope, facing, shade, slope_out, facing_out, shade_out = refs[:7]
    boxes = refs[7 : 7 + SCALES]
    sums, coef, slope_far, facing_far, shade_far_, near_sem, far_sem = refs[7 + SCALES :]
    lat = lax.axis_index("lat")
    n_lat, n_lon = lax.axis_size("lat"), lax.axis_size("lon")
    far = 1 - near_side(lat)
    strips = cols // LANES
    main = rows - HALO
    base = pl.multiple_of(jnp.where(far == 0, HALO, 0), SUB)
    far_base = pl.multiple_of(jnp.where(far == 0, 0, main), SUB)
    done = [
        pltpu.make_async_copy(slope, slope_out.at[pl.ds(base, main), :], near_sem.at[0]),
        pltpu.make_async_copy(shade, shade_out.at[pl.ds(base, main), :], near_sem.at[1]),
        pltpu.make_async_copy(
            facing.at[0], facing_out.at[0, pl.ds(base, main), :], near_sem.at[2]
        ),
        pltpu.make_async_copy(
            facing.at[1], facing_out.at[1, pl.ds(base, main), :], near_sem.at[3]
        ),
    ]
    for copy in done:
        copy.start()
    fill_coef(coef, HALO, lat * rows + far_base, rows * n_lat, cols * n_lon)
    window = Window(
        strips_ref,
        HALO + far_base,
        HALO,
        strips // 4,
        boxes,
        sums,
        coef,
        slope_far,
        facing_far,
        shade_far_,
    )

    def copies(number):
        width = strips // 4 * LANES
        found = []
        for run, start in enumerate(run_starts(number, strips)):
            column = pl.ds(pl.multiple_of(start * LANES, LANES), width)
            here = pl.ds(far_base, HALO)
            for index, (source, target) in enumerate(
                (
                    (slope_far.at[:, column], slope_out.at[here, column]),
                    (shade_far_.at[:, column], shade_out.at[here, column]),
                    (facing_far.at[0, :, column], facing_out.at[0, here, column]),
                    (facing_far.at[1, :, column], facing_out.at[1, here, column]),
                )
            ):
                found.append(
                    pltpu.make_async_copy(source, target, far_sem.at[number, run, index])
                )
        return found

    def half(number, carry):
        window.run(run_starts(number, strips))
        for copy in copies(number):
            copy.start()
        return carry

    lax.fori_loop(0, 2, half, 0)
    for copy in done:
        copy.wait()
    for number in range(2):
        for copy in copies(number):
            copy.wait()


def window_scratch(count, strips):
    width = RUNS * (strips // 4)
    return [
        pltpu.VMEM((2, width, count + row_pad(k), LANES), jnp.float32) for k in range(SCALES)
    ] + [
        pltpu.VMEM((2, width, SUB, LANES), jnp.float32),
        pltpu.VMEM((count, LANES), jnp.float32),
    ]


def local(elevation):
    rows, cols = elevation.shape
    strips = cols // LANES
    main = rows - HALO
    vmem = pl.BlockSpec(memory_space=pltpu.VMEM)
    anywhere = pl.BlockSpec(memory_space=pl.ANY)
    staged = pl.pallas_call(
        functools.partial(gather, rows, cols),
        out_shape=(
            pltpu.VMEM((strips + 2, rows + 2 * HALO, LANES), jnp.float32),
            pltpu.VMEM((main, cols), jnp.float32),
            pltpu.VMEM((2, main, cols), jnp.float32),
            pltpu.VMEM((main, cols), jnp.float32),
        ),
        in_specs=[pl.BlockSpec(memory_space=pltpu.HBM)],
        out_specs=(vmem,) * 4,
        scratch_shapes=window_scratch(main, strips)
        + [
            pltpu.SemaphoreType.DMA((3, strips)),
            pltpu.SemaphoreType.DMA((2, 3)),
            pltpu.SemaphoreType.DMA((2, 3)),
            pltpu.SemaphoreType.DMA((2,)),
            pltpu.SemaphoreType.DMA((2,)),
        ],
        compiler_params=pltpu.CompilerParams(
            collective_id=0, has_side_effects=True, vmem_limit_bytes=54 * 2**20
        ),
    )(elevation)
    return tuple(
        pl.pallas_call(
            functools.partial(shade_far, rows, cols),
            out_shape=(
                jax.ShapeDtypeStruct((rows, cols), jnp.float32),
                jax.ShapeDtypeStruct((2, rows, cols), jnp.float32),
                jax.ShapeDtypeStruct((rows, cols), jnp.float32),
            ),
            in_specs=[vmem] * 4,
            out_specs=(anywhere,) * 3,
            scratch_shapes=window_scratch(HALO, strips)
            + [
                pltpu.VMEM((HALO, cols), jnp.float32),
                pltpu.VMEM((2, HALO, cols), jnp.float32),
                pltpu.VMEM((HALO, cols), jnp.float32),
                pltpu.SemaphoreType.DMA((4,)),
                pltpu.SemaphoreType.DMA((2, RUNS, 4)),
            ],
            compiler_params=pltpu.CompilerParams(vmem_limit_bytes=16 * 2**20),
        )(*staged)
    )


def solution(mesh):
    in_specs = (P("lat", "lon"),)
    out_specs = (P("lat", "lon"), P(None, "lat", "lon"), P("lat", "lon"))
    return jax.shard_map(local, mesh=mesh, in_specs=in_specs, out_specs=out_specs, check_vma=False)
```

profile of v0, /device:TPU:1, one launch (start us, length us, event | category | flops | bytes accessed | tf_op | source)
XLA Modules:
  0.0 26.5 jit_solution(16448720763041036167)
XLA Ops:
  0.6 19.8 %shard_map.38 = (f32[18,384,128]{2,1,0:T(8,128)S(1)}, f32[192,2048]{1,0:T(8,128)S(1)}, f32[2,192,2048]{2,1,0:T(8,128)S(1)}, f32[192,2048]{1,0:T(8,128)S(1)}) custom-call(f32[256,2048]{1,0:T(8,128)} %z_ref.1), custom_call_target="tpu_custom_call" | custom-call | tf_op jit(solution)/shard_map/pallas_call | solution.py:419
  20.4 6.1 %shard_map.39 = (f32[256,2048]{1,0:T(8,128)}, f32[2,256,2048]{2,1,0:T(8,128)}, f32[256,2048]{1,0:T(8,128)}) custom-call(f32[18,384,128]{2,1,0:T(8,128)S(1)} %get-tuple-element.7.refs_0_, f32[192,2048]{1,0:T(8,128)S(1)} %get-tuple-element.8.refs_1_, f32[2,192,2048]{2,1,0:T(8,128)S(1)} %get-tuple-element.9.refs_2_, f32[192,2048]{1,0:T(8,128)S(1)} %get-tuple-element.10.refs_3_), custom_call_target="tpu_custom_call" | custom-call | tf_op jit(solution)/shard_map/pallas_call | solution.py:442
where the time goes:
time: 26.7 us; the launch traced here: 26.5 us
  Pallas kernels  25.9 us (97%)
  between operations  0.64 us (2%)
    pallas_call x1, Pallas kernels, local(): pl.pallas_call(functools.partial(gather, rows, cols), out_shape=(pltpu.VM...  19.8 us
    pallas_call x1, Pallas kernels, local(): pl.pallas_call(functools.partial(shade_far, rows, cols), out_shape=(jax.S...  6.1 us

commit v1 on v0

v1 whole, which is shorter than its diff:
```python
import functools
import math

import jax
import jax.numpy as jnp
from jax import lax
from jax.experimental import pallas as pl
from jax.experimental.pallas import tpu as pltpu
from jax.sharding import PartitionSpec as P

SCALES = 7
HALO = 64
LANES = 128
SUB = 8
RUNS = 2
UNROLL = 4

LIGHT_UP = math.sqrt(0.5)
MESH = pl.DeviceIdType.MESH

ANGLE = (
    1.5707962050889646,
    -0.9999801696091738,
    0.7848538132927688,
    -0.6607586188432167,
    0.5557489578459907,
    -0.42189571811945836,
    0.2501265286961767,
    -0.09607630454800326,
    0.01718536914918157,
)


def row_pad(octave):
    return max(2**octave, SUB)


def rim_hops(strips):
    lon, n_lon = lax.axis_index("lon"), lax.axis_size("lon")
    hops = [(lax.rem(lon + 1, n_lon), 0)]
    if n_lon > 2:
        hops.append((lax.rem(lon + n_lon - 1, n_lon), strips + 1))
    return hops


def east_halo(strips):
    return strips + 1 if lax.axis_size("lon") > 2 else 0


def near_side(lat):
    return 1 - lax.rem(lat, 2)


def fill_coef(coef_ref, count, first_row, total_rows, total_cols):
    for start in range(0, count, SUB):
        position = first_row + start + lax.broadcasted_iota(jnp.int32, (SUB, LANES), 0)
        spacing = jnp.sin((position.astype(jnp.float32) + 0.5) * (math.pi / total_rows)) * (
            2.0 * total_rows / total_cols
        )
        coef_ref[pl.ds(start, SUB), :] = 1.0 / (8.0 * SCALES * spacing)


class Window:
    def __init__(self, strips, rows, columns, far, coef, slope, facing, shade):
        self.strips, self.rows, self.columns = strips, rows, columns
        self.width = columns // 4
        self.coef, self.slope, self.facing, self.shade = coef, slope, facing, shade
        self.top = far == 0
        self.sign = jnp.where(self.top, 1, -1)
        self.lane = lax.broadcasted_iota(jnp.int32, (SUB, LANES), 1)

    def row(self, number):
        return pl.multiple_of(
            jnp.where(self.top, number * SUB, self.rows - SUB - number * SUB), SUB
        )

    def shift(self, octave):
        lag = 2**octave
        moved = self.sign * lag
        return pl.multiple_of(moved, SUB) if lag >= SUB else moved

    def column(self, starts, run, offset, row, shift=0):
        place = pl.ds(HALO + row + shift, SUB)
        strip = starts[run] + offset
        if offset == self.width + 1:
            strip = jnp.where(strip > self.columns, east_halo(self.columns), strip)
        return self.strips[strip, place, :]

    def near(self, starts, row):
        return [
            [self.column(starts, run, k, row) for k in range(self.width + 2)]
            for run in range(RUNS)
        ]

    def box(self, starts, row, octave, near, shift):
        lag = 2**octave
        boxes, shifted = [], []
        for run, z in enumerate(near):
            pair = []
            for k in range(self.width + 2):
                total = z[k] + self.column(starts, run, k, row, shift)
                pair.append(total * (1.0 / lag) if octave else total)
            ahead = [pltpu.roll(v, LANES - lag, 1) for v in pair]
            if 2 * lag == LANES:
                plus = [
                    jnp.where(self.lane < lag, ahead[k], ahead[k + 1])
                    for k in range(self.width + 1)
                ]
                boxes += [pair[k + 1] + plus[k + 1] for k in range(self.width)]
                shifted += [pair[k + 1] + plus[k] for k in range(self.width)]
            else:
                behind = [pltpu.roll(v, lag, 1) for v in pair]
                for k in range(1, self.width + 1):
                    plus = jnp.where(self.lane < LANES - lag, ahead[k], ahead[k + 1])
                    minus = jnp.where(self.lane >= lag, behind[k], behind[k - 1])
                    boxes.append(pair[k] + plus)
                    shifted.append(pair[k] + minus)
        return boxes, shifted

    def add(self, lags, starts, row):
        near = self.near(starts, row)
        count = RUNS * self.width
        first = second = None
        for octave in range(SCALES):
            shift = self.shift(octave)
            boxes, shifted = self.box(starts, row, octave, near, shift)
            here = row_pad(octave) + row
            for k in range(count):
                lags[octave][0, k, pl.ds(pl.multiple_of(here, SUB), SUB), :] = boxes[k]
                lags[octave][1, k, pl.ds(pl.multiple_of(here, SUB), SUB), :] = shifted[k]
            past = pl.ds(here - shift, SUB)
            u = [boxes[k] - lags[octave][1, k, past, :] for k in range(count)]
            v = [lags[octave][0, k, past, :] - shifted[k] for k in range(count)]
            first = u if first is None else [a + b for a, b in zip(first, u)]
            second = v if second is None else [a + b for a, b in zip(second, v)]
        return first, second

    def finish(self, starts, row, first, second):
        rows = pl.ds(pl.multiple_of(row, SUB), SUB)
        coef = self.coef[rows, :]
        turn = jnp.where(self.top, 1.0, -1.0) * (1.0 / (8.0 * SCALES))
        for k in range(RUNS * self.width):
            run, within = divmod(k, self.width)
            column = pl.ds(pl.multiple_of((starts[run] + within) * LANES, LANES), LANES)
            grad_east = (first[k] + second[k]) * coef
            grad_north = (second[k] - first[k]) * turn
            squared = grad_east * grad_east + grad_north * grad_north
            inverse = lax.rsqrt(1.0 + squared)
            sine = squared * lax.rsqrt(jnp.maximum(squared, 1e-37)) * inverse
            ratio = jnp.full_like(inverse, ANGLE[-1])
            for term in ANGLE[-2::-1]:
                ratio = ratio * inverse + term
            self.slope[rows, column] = sine * ratio
            self.facing[0, rows, column] = -grad_east * inverse
            self.facing[1, rows, column] = -grad_north * inverse
            tilt = 0.5 * (grad_east - grad_north) + LIGHT_UP
            self.shade[rows, column] = jnp.maximum(tilt * inverse, 0.0)


def run_starts(half, strips):
    quarter = strips // 4
    return (
        jnp.where(half == 0, quarter, 0),
        jnp.where(half == 0, 2 * quarter, 3 * quarter),
    )


def gather(rows, cols, z_ref, strips_ref, part, slope, facing, shade, *scratch):
    lags, (rim, coef, load_sem, send_sem, recv_sem, rim_send, rim_recv) = (
        scratch[:SCALES],
        scratch[SCALES:],
    )
    lat, lon = lax.axis_index("lat"), lax.axis_index("lon")
    n_lat, n_lon = lax.axis_size("lat"), lax.axis_size("lon")
    strips = cols // LANES
    hops = rim_hops(strips)
    width = strips // 4
    count = RUNS * width
    near = near_side(lat)
    far = 1 - near
    exists = (lat > 0, lat < n_lat - 1)
    far_exists = jnp.where(far == 0, exists[0], exists[1])
    far_lat = jnp.where(far == 0, lat - 1, lat + 1)
    near_lat = jnp.where(near == 0, lat - 1, lat + 1)

    def edge(side):
        return pl.multiple_of(jnp.where(side == 0, 0, rows - HALO), SUB)

    def halo(side):
        return pl.multiple_of(jnp.where(side == 0, 0, HALO + rows), SUB)

    def loads_of(number):
        start, size = ((edge(far), HALO), (edge(near), HALO), (HALO, rows - 2 * HALO))[number]
        return [
            pltpu.make_async_copy(
                z_ref.at[pl.ds(start, size), pl.ds(strip * LANES, LANES)],
                strips_ref.at[1 + strip, pl.ds(HALO + start, size), :],
                load_sem.at[number, strip],
            )
            for strip in range(strips)
        ]

    for number in range(3):
        for load in loads_of(number):
            load.start()

    barrier = pltpu.get_barrier_semaphore()

    @pl.when(far_exists)
    def _():
        for other in [lon] + [hop for hop, _ in hops]:
            pl.semaphore_signal(barrier, inc=1, device_id=(far_lat, other), device_id_type=MESH)

    for other, _ in hops:
        pl.semaphore_signal(barrier, inc=1, device_id=(lat, other), device_id_type=MESH)
    for other in [lon] + [hop for hop, _ in hops]:
        pl.semaphore_signal(barrier, inc=1, device_id=(near_lat, other), device_id_type=MESH)

    main = rows - HALO
    base = pl.multiple_of(jnp.where(far == 0, HALO, 0), SUB)
    fill_coef(coef, main, lat * rows + base, rows * n_lat, cols * n_lon)
    for load in loads_of(0):
        load.wait()
    greeted = 1 + len(hops)
    pl.semaphore_wait(barrier, greeted + len(hops) + greeted * far_exists.astype(jnp.int32))

    def lat_copy(distant):
        side, other = (far, far_lat) if distant else (near, near_lat)
        return pltpu.make_async_remote_copy(
            src_ref=strips_ref.at[pl.ds(1, strips), pl.ds(HALO + edge(side), HALO), :],
            dst_ref=strips_ref.at[pl.ds(1, strips), pl.ds(halo(1 - side), HALO), :],
            send_sem=send_sem.at[distant, 0],
            recv_sem=recv_sem.at[distant, 0],
            device_id=(other, lon),
            device_id_type=MESH,
        )

    def corner_copy(distant, index):
        side, other = (far, far_lat) if distant else (near, near_lat)
        hop, target = hops[index]
        return pltpu.make_async_remote_copy(
            src_ref=rim.at[pl.ds(edge(side), HALO), :],
            dst_ref=strips_ref.at[target, pl.ds(halo(1 - side), HALO), :],
            send_sem=send_sem.at[distant, 1 + index],
            recv_sem=recv_sem.at[distant, 1 + index],
            device_id=(other, hop),
            device_id_type=MESH,
        )

    def rim_copy(index):
        hop, target = hops[index]
        return pltpu.make_async_remote_copy(
            src_ref=rim,
            dst_ref=strips_ref.at[target, pl.ds(HALO, rows), :],
            send_sem=rim_send.at[index],
            recv_sem=rim_recv.at[index],
            device_id=(lat, hop),
            device_id_type=MESH,
        )

    def arrived(distant, kind):
        here = pl.ds(halo(far if distant else near), HALO)
        if kind == 0:
            place = strips_ref.at[pl.ds(1, strips), here, :]
        else:
            place = strips_ref.at[hops[kind - 1][1], here, :]
        pltpu.make_async_remote_copy(
            src_ref=place,
            dst_ref=place,
            send_sem=send_sem.at[distant, kind],
            recv_sem=recv_sem.at[distant, kind],
            device_id=(lat, hops[0][0]),
            device_id_type=MESH,
        ).wait_recv()

    @pl.when(far_exists)
    def _():
        lat_copy(1).start()

    for load in loads_of(1):
        load.wait()
    lat_copy(0).start()
    for load in loads_of(2):
        load.wait()
    lane = lax.broadcasted_iota(jnp.int32, (SUB, LANES), 1)
    for start in range(0, rows, SUB):
        here = pl.ds(HALO + start, SUB)
        rim[pl.ds(start, SUB), :] = jnp.where(
            lane < HALO, strips_ref[1, here, :], strips_ref[strips, here, :]
        )

    for octave in range(SCALES):
        pad = row_pad(octave)
        first = pl.multiple_of(jnp.where(far == 0, 0, pad + rows), SUB)
        for k in range(count):
            for start in range(0, pad, SUB):
                for which in range(2):
                    lags[octave][which, k, pl.ds(first + start, SUB), :] = jnp.zeros(
                        (SUB, LANES), jnp.float32
                    )

    for index in range(len(hops)):
        rim_copy(index).start()
        corner_copy(0, index).start()

    @pl.when(far_exists)
    def _():
        for index in range(len(hops)):
            corner_copy(1, index).start()

    window = Window(strips_ref, rows, strips, far, coef, slope, facing, shade)
    far_base = pl.multiple_of(jnp.where(far == 0, 0, main), SUB)

    def half(number, carry):
        @pl.when(number == 1)
        def _():
            for index in range(len(hops)):
                rim_copy(index).wait_recv()
                arrived(0, 1 + index)

        starts = run_starts(number, strips)

        def partly(block, carry):
            for inner in range(UNROLL):
                row = window.row(block * UNROLL + inner)
                found = window.add(lags, starts, row)
                rows_here = pl.ds(pl.multiple_of(row - far_base, SUB), SUB)
                for which in range(2):
                    for k in range(count):
                        run, within = divmod(k, width)
                        part[which, starts[run] + within, rows_here, :] = found[which][k]
            return carry

        def fully(block, carry):
            for inner in range(UNROLL):
                row = window.row(block * UNROLL + inner)
                window.finish(starts, row - base, *window.add(lags, starts, row))
            return carry

        size = UNROLL * SUB
        lax.fori_loop(0, HALO // size, partly, 0)
        lax.fori_loop(HALO // size, (rows - HALO) // size, fully, 0)

        @pl.when(number == 0)
        def _():
            arrived(0, 0)

        lax.fori_loop((rows - HALO) // size, rows // size, fully, 0)
        return carry

    lax.fori_loop(0, 2, half, 0)

    for pole in range(2):

        @pl.when(jnp.logical_and(jnp.logical_not(far_exists), far == pole))
        def _():
            first = HALO if pole == 0 else HALO + rows - SUB
            pick = 0 if pole == 0 else SUB - 1
            fill = 0 if pole == 0 else HALO + rows

            def repeat(strip, carry):
                row = strips_ref[strip, pl.ds(first, SUB), :][pick : pick + 1]
                block = jnp.broadcast_to(row, (SUB, LANES))
                for k in range(HALO // SUB):
                    strips_ref[strip, pl.ds(fill + k * SUB, SUB), :] = block
                return carry

            lax.fori_loop(0, strips_ref.shape[0], repeat, 0)

    lat_copy(0).wait_send()
    for index in range(len(hops)):
        rim_copy(index).wait_send()
        corner_copy(0, index).wait_send()

    @pl.when(far_exists)
    def _():
        lat_copy(1).wait_send()
        arrived(1, 0)
        for index in range(len(hops)):
            corner_copy(1, index).wait_send()
            arrived(1, 1 + index)


def shade_far(rows, cols, *refs):
    strips_ref, part, slope, facing, shade, slope_out, facing_out, shade_out = refs[:8]
    coef, slope_far, facing_far, shade_far_, near_sem, far_sem = refs[8:]
    lat = lax.axis_index("lat")
    n_lat, n_lon = lax.axis_size("lat"), lax.axis_size("lon")
    far = 1 - near_side(lat)
    strips = cols // LANES
    width = strips // 4
    count = RUNS * width
    main = rows - HALO
    base = pl.multiple_of(jnp.where(far == 0, HALO, 0), SUB)
    far_base = pl.multiple_of(jnp.where(far == 0, 0, main), SUB)
    done = [
        pltpu.make_async_copy(source, target, near_sem.at[index])
        for index, (source, target) in enumerate(
            (
                (slope, slope_out.at[pl.ds(base, main), :]),
                (shade, shade_out.at[pl.ds(base, main), :]),
                (facing.at[0], facing_out.at[0, pl.ds(base, main), :]),
                (facing.at[1], facing_out.at[1, pl.ds(base, main), :]),
            )
        )
    ]
    for copy in done:
        copy.start()
    fill_coef(coef, HALO, lat * rows + far_base, rows * n_lat, cols * n_lon)
    window = Window(strips_ref, rows, strips, far, coef, slope_far, facing_far, shade_far_)
    sublane = lax.broadcasted_iota(jnp.int32, (SUB, LANES), 0)

    def copies(number):
        found = []
        for run, start in enumerate(run_starts(number, strips)):
            column = pl.ds(pl.multiple_of(start * LANES, LANES), width * LANES)
            here = pl.ds(far_base, HALO)
            for index, (source, target) in enumerate(
                (
                    (slope_far.at[:, column], slope_out.at[here, column]),
                    (shade_far_.at[:, column], shade_out.at[here, column]),
                    (facing_far.at[0, :, column], facing_out.at[0, here, column]),
                    (facing_far.at[1, :, column], facing_out.at[1, here, column]),
                )
            ):
                found.append(
                    pltpu.make_async_copy(source, target, far_sem.at[number, run, index])
                )
        return found

    def half(number, carry):
        starts = run_starts(number, strips)
        for step in range(HALO // SUB):
            row = window.row(step)
            local_row = pl.multiple_of(row - far_base, SUB)
            first, second = [
                [
                    part[which, starts[k // width] + k % width, pl.ds(local_row, SUB), :]
                    for k in range(count)
                ]
                for which in range(2)
            ]
            near = window.near(starts, row)
            for octave in range(SCALES):
                lag = 2**octave
                if row_pad(octave) <= step * SUB:
                    continue
                boxes, shifted = window.box(starts, row, octave, near, -window.shift(octave))
                if lag < SUB:
                    beyond = jnp.logical_or(
                        jnp.logical_and(far == 0, sublane < lag),
                        jnp.logical_and(far == 1, sublane >= SUB - lag),
                    )
                    boxes = [jnp.where(beyond, v, 0.0) for v in boxes]
                    shifted = [jnp.where(beyond, v, 0.0) for v in shifted]
                first = [a - b for a, b in zip(first, shifted)]
                second = [a + b for a, b in zip(second, boxes)]
            window.finish(starts, local_row, first, second)
        for copy in copies(number):
            copy.start()
        return carry

    lax.fori_loop(0, 2, half, 0)
    for copy in done:
        copy.wait()
    for number in range(2):
        for copy in copies(number):
            copy.wait()


def local(elevation):
    rows, cols = elevation.shape
    strips = cols // LANES
    count = RUNS * (strips // 4)
    hops = 1 if lax.axis_size("lon") == 2 else 2
    main = rows - HALO
    vmem = pl.BlockSpec(memory_space=pltpu.VMEM)
    anywhere = pl.BlockSpec(memory_space=pl.ANY)
    staged = pl.pallas_call(
        functools.partial(gather, rows, cols),
        out_shape=(
            pltpu.VMEM((strips + hops, rows + 2 * HALO, LANES), jnp.float32),
            pltpu.VMEM((2, strips, HALO, LANES), jnp.float32),
            pltpu.VMEM((main, cols), jnp.float32),
            pltpu.VMEM((2, main, cols), jnp.float32),
            pltpu.VMEM((main, cols), jnp.float32),
        ),
        in_specs=[anywhere],
        out_specs=(vmem,) * 5,
        scratch_shapes=[
            pltpu.VMEM((2, count, rows + 2 * row_pad(k), LANES), jnp.float32)
            for k in range(SCALES)
        ]
        + [
            pltpu.VMEM((rows, LANES), jnp.float32),
            pltpu.VMEM((main, LANES), jnp.float32),
            pltpu.SemaphoreType.DMA((3, strips)),
            pltpu.SemaphoreType.DMA((2, 1 + hops)),
            pltpu.SemaphoreType.DMA((2, 1 + hops)),
            pltpu.SemaphoreType.DMA((hops,)),
            pltpu.SemaphoreType.DMA((hops,)),
        ],
        compiler_params=pltpu.CompilerParams(
            collective_id=0, has_side_effects=True, vmem_limit_bytes=52 * 2**20
        ),
    )(elevation)
    return tuple(
        pl.pallas_call(
            functools.partial(shade_far, rows, cols),
            out_shape=(
                jax.ShapeDtypeStruct((rows, cols), jnp.float32),
                jax.ShapeDtypeStruct((2, rows, cols), jnp.float32),
                jax.ShapeDtypeStruct((rows, cols), jnp.float32),
            ),
            in_specs=[vmem] * 5,
            out_specs=(anywhere,) * 3,
            scratch_shapes=[
                pltpu.VMEM((HALO, LANES), jnp.float32),
                pltpu.VMEM((HALO, cols), jnp.float32),
                pltpu.VMEM((2, HALO, cols), jnp.float32),
                pltpu.VMEM((HALO, cols), jnp.float32),
                pltpu.SemaphoreType.DMA((4,)),
                pltpu.SemaphoreType.DMA((2, RUNS, 4)),
            ],
            compiler_params=pltpu.CompilerParams(vmem_limit_bytes=16 * 2**20),
        )(*staged)
    )


def solution(mesh):
    in_specs = (P("lat", "lon"),)
    out_specs = (P("lat", "lon"), P(None, "lat", "lon"), P("lat", "lon"))
    return jax.shard_map(local, mesh=mesh, in_specs=in_specs, out_specs=out_specs, check_vma=False)
```

time: 26.7 us -> 22.6 us (0.85)
  Pallas kernels: 25.9 us -> 21.8 us
    pallas_call x1, Pallas kernels: 6.1 us -> 3.46 us  [local(): pl.pallas_call(functools.partial(shade_far, rows, cols), out_shape=(jax.S...]
    pallas_call x1, Pallas kernels: 19.8 us -> 18.3 us  [local(): pl.pallas_call(functools.partial(gather, rows, cols), out_shape=(pltpu.VM...]
where the time goes in v1:
time: 22.6 us; the launch traced here: 22.4 us
  Pallas kernels  21.8 us (96%)
  between operations  0.64 us (3%)
    pallas_call x1, Pallas kernels, local(): pl.pallas_call(functools.partial(gather, rows, cols), out_shape=(pltpu.VM...  18.3 us
    pallas_call x1, Pallas kernels, local(): pl.pallas_call(functools.partial(shade_far, rows, cols), out_shape=(jax.S...  3.46 us

profile of v1, /device:TPU:1, one launch (start us, length us, event | category | flops | bytes accessed | tf_op | source)
XLA Modules:
  0.0 22.4 jit_solution(11911071179766665243)
XLA Ops:
  0.6 18.3 %shard_map.38 = (f32[17,384,128]{2,1,0:T(8,128)S(1)}, f32[2,16,64,128]{3,2,1,0:T(8,128)S(1)}, f32[192,2048]{1,0:T(8,128)S(1)}, f32[2,192,2048]{2,1,0:T(8,128)S(1)}, f32[192,2048]{1,0:T(8,128)S(1)}) custom-call(f32[256,2048]{1,0:T(8,128)} %z_ref.1), custom_call_target="tpu_custom_call" | custom-call | tf_op jit(solution)/shard_map/pallas_call | solution.py:479
  19.0 3.5 %shard_map.39 = (f32[256,2048]{1,0:T(8,128)}, f32[2,256,2048]{2,1,0:T(8,128)}, f32[256,2048]{1,0:T(8,128)}) custom-call(f32[17,384,128]{2,1,0:T(8,128)S(1)} %get-tuple-element.8.refs_0_, f32[2,16,64,128]{3,2,1,0:T(8,128)S(1)} %get-tuple-element.9.refs_1_, f32[192,2048]{1,0:T(8,128)S(1)} %get-tuple-element.10.refs_2_, ...), custom_call_target="tpu_custom_call" | custom-call | tf_op jit(solution)/shard_map/pallas_call | solution.py:508

commit v2 on v1

--- a/solution.py
+++ b/solution.py
@@ -31,6 +31,10 @@
 )
 
 
+def spread(rows):
+    return rows + (-rows // SUB + 1) % 4 * SUB
+
+
 def row_pad(octave):
     return max(2**octave, SUB)
 
@@ -86,16 +90,16 @@
             strip = jnp.where(strip > self.columns, east_halo(self.columns), strip)
         return self.strips[strip, place, :]
 
-    def near(self, starts, row):
+    def near(self, starts, row, runs):
         return [
-            [self.column(starts, run, k, row) for k in range(self.width + 2)]
-            for run in range(RUNS)
+            (run, [self.column(starts, run, k, row) for k in range(self.width + 2)])
+            for run in runs
         ]
 
     def box(self, starts, row, octave, near, shift):
         lag = 2**octave
         boxes, shifted = [], []
-        for run, z in enumerate(near):
+        for run, z in near:
             pair = []
             for k in range(self.width + 2):
                 total = z[k] + self.column(starts, run, k, row, shift)
@@ -117,30 +121,31 @@
                     shifted.append(pair[k] + minus)
         return boxes, shifted
 
-    def add(self, lags, starts, row):
-        near = self.near(starts, row)
-        count = RUNS * self.width
+    def add(self, lags, starts, row, run):
+        near = self.near(starts, row, [run])
+        count = self.width
+        low = run * self.width
         first = second = None
         for octave in range(SCALES):
             shift = self.shift(octave)
             boxes, shifted = self.box(starts, row, octave, near, shift)
             here = row_pad(octave) + row
             for k in range(count):
-                lags[octave][0, k, pl.ds(pl.multiple_of(here, SUB), SUB), :] = boxes[k]
-                lags[octave][1, k, pl.ds(pl.multiple_of(here, SUB), SUB), :] = shifted[k]
+                lags[octave][0, low + k, pl.ds(pl.multiple_of(here, SUB), SUB), :] = boxes[k]
+                lags[octave][1, low + k, pl.ds(pl.multiple_of(here, SUB), SUB), :] = shifted[k]
             past = pl.ds(here - shift, SUB)
-            u = [boxes[k] - lags[octave][1, k, past, :] for k in range(count)]
-            v = [lags[octave][0, k, past, :] - shifted[k] for k in range(count)]
+            u = [boxes[k] - lags[octave][1, low + k, past, :] for k in range(count)]
+            v = [lags[octave][0, low + k, past, :] - shifted[k] for k in range(count)]
             first = u if first is None else [a + b for a, b in zip(first, u)]
             second = v if second is None else [a + b for a, b in zip(second, v)]
         return first, second
 
-    def finish(self, starts, row, first, second):
+    def finish(self, starts, row, first, second, runs=(0, 1)):
         rows = pl.ds(pl.multiple_of(row, SUB), SUB)
         coef = self.coef[rows, :]
         turn = jnp.where(self.top, 1.0, -1.0) * (1.0 / (8.0 * SCALES))
-        for k in range(RUNS * self.width):
-            run, within = divmod(k, self.width)
+        for k in range(len(runs) * self.width):
+            run, within = runs[k // self.width], k % self.width
             column = pl.ds(pl.multiple_of((starts[run] + within) * LANES, LANES), LANES)
             grad_east = (first[k] + second[k]) * coef
             grad_north = (second[k] - first[k]) * turn
@@ -151,8 +156,9 @@
             for term in ANGLE[-2::-1]:
                 ratio = ratio * inverse + term
             self.slope[rows, column] = sine * ratio
-            self.facing[0, rows, column] = -grad_east * inverse
-            self.facing[1, rows, column] = -grad_north * inverse
+            turned = -inverse
+            self.facing[0, rows, column] = grad_east * turned
+            self.facing[1, rows, column] = grad_north * turned
             tilt = 0.5 * (grad_east - grad_north) + LIGHT_UP
             self.shade[rows, column] = jnp.maximum(tilt * inverse, 0.0)
 
@@ -166,7 +172,7 @@
 
 
 def gather(rows, cols, z_ref, strips_ref, part, slope, facing, shade, *scratch):
-    lags, (rim, coef, load_sem, send_sem, recv_sem, rim_send, rim_recv) = (
+    lags, (rim, coef, greeted, load_sem, send_sem, recv_sem, rim_send, rim_recv) = (
         scratch[:SCALES],
         scratch[SCALES:],
     )
@@ -208,21 +214,20 @@
 
     @pl.when(far_exists)
     def _():
-        for other in [lon] + [hop for hop, _ in hops]:
-            pl.semaphore_signal(barrier, inc=1, device_id=(far_lat, other), device_id_type=MESH)
-
-    for other, _ in hops:
-        pl.semaphore_signal(barrier, inc=1, device_id=(lat, other), device_id_type=MESH)
-    for other in [lon] + [hop for hop, _ in hops]:
-        pl.semaphore_signal(barrier, inc=1, device_id=(near_lat, other), device_id_type=MESH)
+        pl.semaphore_signal(barrier, inc=1, device_id=(far_lat, lon), device_id_type=MESH)
+
+    for hop, _ in hops:
+        pl.semaphore_signal(barrier, inc=1, device_id=(lat, hop), device_id_type=MESH)
+    pl.semaphore_signal(barrier, inc=1, device_id=(near_lat, lon), device_id_type=MESH)
 
     main = rows - HALO
     base = pl.multiple_of(jnp.where(far == 0, HALO, 0), SUB)
     fill_coef(coef, main, lat * rows + base, rows * n_lat, cols * n_lon)
     for load in loads_of(0):
         load.wait()
-    greeted = 1 + len(hops)
-    pl.semaphore_wait(barrier, greeted + len(hops) + greeted * far_exists.astype(jnp.int32))
+    pl.semaphore_wait(barrier, 1 + len(hops) + far_exists.astype(jnp.int32))
+    for hop, _ in hops:
+        pl.semaphore_signal(greeted, inc=1, device_id=(lat, hop), device_id_type=MESH)
 
     def lat_copy(distant):
         side, other = (far, far_lat) if distant else (near, near_lat)
@@ -301,6 +306,8 @@
 
     for index in range(len(hops)):
         rim_copy(index).start()
+    pl.semaphore_wait(greeted, len(hops))
+    for index in range(len(hops)):
         corner_copy(0, index).start()
 
     @pl.when(far_exists)
@@ -323,29 +330,31 @@
         def partly(block, carry):
             for inner in range(UNROLL):
                 row = window.row(block * UNROLL + inner)
-                found = window.add(lags, starts, row)
                 rows_here = pl.ds(pl.multiple_of(row - far_base, SUB), SUB)
-                for which in range(2):
-                    for k in range(count):
-                        run, within = divmod(k, width)
-                        part[which, starts[run] + within, rows_here, :] = found[which][k]
+                for run in range(RUNS):
+                    found = window.add(lags, starts, row, run)
+                    for which in range(2):
+                        for k in range(width):
+                            part[which, starts[run] + k, rows_here, :] = found[which][k]
             return carry
 
         def fully(block, carry):
             for inner in range(UNROLL):
                 row = window.row(block * UNROLL + inner)
-                window.finish(starts, row - base, *window.add(lags, starts, row))
+                for run in range(RUNS):
+                    window.finish(
+                        starts, row - base, *window.add(lags, starts, row, run), runs=(run,)
+                    )
             return carry
 
         size = UNROLL * SUB
         lax.fori_loop(0, HALO // size, partly, 0)
-        lax.fori_loop(HALO // size, (rows - HALO) // size, fully, 0)
 
         @pl.when(number == 0)
         def _():
             arrived(0, 0)
 
-        lax.fori_loop((rows - HALO) // size, rows // size, fully, 0)
+        lax.fori_loop(HALO // size, rows // size, fully, 0)
         return carry
 
     lax.fori_loop(0, 2, half, 0)
@@ -440,7 +449,7 @@
                 ]
                 for which in range(2)
             ]
-            near = window.near(starts, row)
+            near = window.near(starts, row, range(RUNS))
             for octave in range(SCALES):
                 lag = 2**octave
                 if row_pad(octave) <= step * SUB:
@@ -479,7 +488,7 @@
     staged = pl.pallas_call(
         functools.partial(gather, rows, cols),
         out_shape=(
-            pltpu.VMEM((strips + hops, rows + 2 * HALO, LANES), jnp.float32),
+            pltpu.VMEM((strips + hops, spread(rows + 2 * HALO), LANES), jnp.float32),
             pltpu.VMEM((2, strips, HALO, LANES), jnp.float32),
             pltpu.VMEM((main, cols), jnp.float32),
             pltpu.VMEM((2, main, cols), jnp.float32),
@@ -488,12 +497,13 @@
         in_specs=[anywhere],
         out_specs=(vmem,) * 5,
         scratch_shapes=[
-            pltpu.VMEM((2, count, rows + 2 * row_pad(k), LANES), jnp.float32)
+            pltpu.VMEM((2, count, spread(rows + 2 * row_pad(k)), LANES), jnp.float32)
             for k in range(SCALES)
         ]
         + [
             pltpu.VMEM((rows, LANES), jnp.float32),
             pltpu.VMEM((main, LANES), jnp.float32),
+            pltpu.SemaphoreType.REGULAR,
             pltpu.SemaphoreType.DMA((3, strips)),
             pltpu.SemaphoreType.DMA((2, 1 + hops)),
             pltpu.SemaphoreType.DMA((2, 1 + hops)),

time: 22.6 us -> 21.7 us (0.960)
  the two profiles are of different devices: /device:TPU:1 before, /device:TPU:9 now
where the time goes in v2:
time: 21.7 us; the launch traced here: 21.5 us
  Pallas kernels  20.9 us (96%)
  between operations  0.64 us (3%)
    pallas_call x1, Pallas kernels, local(): pl.pallas_call(functools.partial(gather, rows, cols), out_shape=(pltpu.VM...  17.4 us
    pallas_call x1, Pallas kernels, local(): pl.pallas_call(functools.partial(shade_far, rows, cols), out_shape=(jax.S...  3.46 us

profile of v2, /device:TPU:9, one launch (start us, length us, event | category | flops | bytes accessed | tf_op | source)
XLA Modules:
  0.0 21.5 jit_solution(14457374944233633877)
XLA Ops:
  0.6 17.4 %shard_map.38 = (f32[17,392,128]{2,1,0:T(8,128)S(1)}, f32[2,16,64,128]{3,2,1,0:T(8,128)S(1)}, f32[192,2048]{1,0:T(8,128)S(1)}, f32[2,192,2048]{2,1,0:T(8,128)S(1)}, f32[192,2048]{1,0:T(8,128)S(1)}) custom-call(f32[256,2048]{1,0:T(8,128)} %z_ref.1), custom_call_target="tpu_custom_call" | custom-call | tf_op jit(solution)/shard_map/pallas_call | solution.py:488
  18.0 3.5 %shard_map.39 = (f32[256,2048]{1,0:T(8,128)}, f32[2,256,2048]{2,1,0:T(8,128)}, f32[256,2048]{1,0:T(8,128)}) custom-call(f32[17,392,128]{2,1,0:T(8,128)S(1)} %get-tuple-element.8.refs_0_, f32[2,16,64,128]{3,2,1,0:T(8,128)S(1)} %get-tuple-element.9.refs_1_, f32[192,2048]{1,0:T(8,128)S(1)} %get-tuple-element.10.refs_2_, ...), custom_call_target="tpu_custom_call" | custom-call | tf_op jit(solution)/shard_map/pallas_call | solution.py:518

commit v3 on v2

--- a/solution.py
+++ b/solution.py
@@ -172,7 +172,18 @@
 
 
 def gather(rows, cols, z_ref, strips_ref, part, slope, facing, shade, *scratch):
-    lags, (rim, coef, greeted, load_sem, send_sem, recv_sem, rim_send, rim_recv) = (
+    lags, (
+        rim,
+        coef,
+        greeted,
+        load_sem,
+        lat_send,
+        lat_recv,
+        send_sem,
+        recv_sem,
+        rim_send,
+        rim_recv,
+    ) = (
         scratch[:SCALES],
         scratch[SCALES:],
     )
@@ -206,36 +217,51 @@
             for strip in range(strips)
         ]
 
+    barrier = pltpu.get_barrier_semaphore()
+
+    @pl.when(far_exists)
+    def _():
+        pl.semaphore_signal(barrier, inc=1, device_id=(far_lat, lon), device_id_type=MESH)
+
+    pl.semaphore_signal(barrier, inc=1, device_id=(near_lat, lon), device_id_type=MESH)
+
     for number in range(3):
         for load in loads_of(number):
             load.start()
-
-    barrier = pltpu.get_barrier_semaphore()
-
-    @pl.when(far_exists)
-    def _():
-        pl.semaphore_signal(barrier, inc=1, device_id=(far_lat, lon), device_id_type=MESH)
-
-    for hop, _ in hops:
-        pl.semaphore_signal(barrier, inc=1, device_id=(lat, hop), device_id_type=MESH)
-    pl.semaphore_signal(barrier, inc=1, device_id=(near_lat, lon), device_id_type=MESH)
 
     main = rows - HALO
     base = pl.multiple_of(jnp.where(far == 0, HALO, 0), SUB)
     fill_coef(coef, main, lat * rows + base, rows * n_lat, cols * n_lon)
     for load in loads_of(0):
         load.wait()
-    pl.semaphore_wait(barrier, 1 + len(hops) + far_exists.astype(jnp.int32))
-    for hop, _ in hops:
-        pl.semaphore_signal(greeted, inc=1, device_id=(lat, hop), device_id_type=MESH)
-
-    def lat_copy(distant):
+    odd = lax.rem(lon, 2)
+    leads = odd == 0
+    follows = odd == 1
+    pl.semaphore_wait(barrier, 1 + far_exists.astype(jnp.int32) + len(hops) * odd)
+
+    @pl.when(leads)
+    def _():
+        for hop, _ in hops:
+            pl.semaphore_signal(barrier, inc=1, device_id=(lat, hop), device_id_type=MESH)
+
+    @pl.when(follows)
+    def _():
+        for hop, _ in hops:
+            pl.semaphore_signal(greeted, inc=1, device_id=(lat, hop), device_id_type=MESH)
+
+
+    quarter = strips // 4
+    pieces = ((1, quarter), (1 + quarter, strips - quarter))
+
+    def lat_copy(distant, piece):
         side, other = (far, far_lat) if distant else (near, near_lat)
+        part_ = pl.ds(*piece)
+        index = pieces.index(piece)
         return pltpu.make_async_remote_copy(
-            src_ref=strips_ref.at[pl.ds(1, strips), pl.ds(HALO + edge(side), HALO), :],
-            dst_ref=strips_ref.at[pl.ds(1, strips), pl.ds(halo(1 - side), HALO), :],
-            send_sem=send_sem.at[distant, 0],
-            recv_sem=recv_sem.at[distant, 0],
+            src_ref=strips_ref.at[part_, pl.ds(HALO + edge(side), HALO), :],
+            dst_ref=strips_ref.at[part_, pl.ds(halo(1 - side), HALO), :],
+            send_sem=lat_send.at[distant, index],
+            recv_sem=lat_recv.at[distant, index],
             device_id=(other, lon),
             device_id_type=MESH,
         )
@@ -246,8 +272,8 @@
         return pltpu.make_async_remote_copy(
             src_ref=rim.at[pl.ds(edge(side), HALO), :],
             dst_ref=strips_ref.at[target, pl.ds(halo(1 - side), HALO), :],
-            send_sem=send_sem.at[distant, 1 + index],
-            recv_sem=recv_sem.at[distant, 1 + index],
+            send_sem=send_sem.at[distant, index],
+            recv_sem=recv_sem.at[distant, index],
             device_id=(other, hop),
             device_id_type=MESH,
         )
@@ -263,28 +289,31 @@
             device_id_type=MESH,
         )
 
-    def arrived(distant, kind):
+    def arrived(distant, piece=None, index=0):
         here = pl.ds(halo(far if distant else near), HALO)
-        if kind == 0:
-            place = strips_ref.at[pl.ds(1, strips), here, :]
+        if piece is None:
+            place = strips_ref.at[hops[index][1], here, :]
+            sends, receives = send_sem, recv_sem
         else:
-            place = strips_ref.at[hops[kind - 1][1], here, :]
+            place = strips_ref.at[pl.ds(*piece), here, :]
+            sends, receives, index = lat_send, lat_recv, pieces.index(piece)
         pltpu.make_async_remote_copy(
             src_ref=place,
             dst_ref=place,
-            send_sem=send_sem.at[distant, kind],
-            recv_sem=recv_sem.at[distant, kind],
+            send_sem=sends.at[distant, index],
+            recv_sem=receives.at[distant, index],
             device_id=(lat, hops[0][0]),
             device_id_type=MESH,
         ).wait_recv()
 
     @pl.when(far_exists)
     def _():
-        lat_copy(1).start()
+        lat_copy(1, pieces[0]).start()
 
     for load in loads_of(1):
         load.wait()
-    lat_copy(0).start()
+    for piece in pieces:
+        lat_copy(0, piece).start()
     for load in loads_of(2):
         load.wait()
     lane = lax.broadcasted_iota(jnp.int32, (SUB, LANES), 1)
@@ -304,16 +333,21 @@
                         (SUB, LANES), jnp.float32
                     )
 
-    for index in range(len(hops)):
-        rim_copy(index).start()
-    pl.semaphore_wait(greeted, len(hops))
-    for index in range(len(hops)):
-        corner_copy(0, index).start()
+    def send_rims():
+        for index in range(len(hops)):
+            rim_copy(index).start()
+            corner_copy(0, index).start()
+
+        @pl.when(far_exists)
+        def _():
+            for index in range(len(hops)):
+                corner_copy(1, index).start()
+
+    pl.when(follows)(send_rims)
 
     @pl.when(far_exists)
     def _():
-        for index in range(len(hops)):
-            corner_copy(1, index).start()
+        lat_copy(1, pieces[1]).start()
 
     window = Window(strips_ref, rows, strips, far, coef, slope, facing, shade)
     far_base = pl.multiple_of(jnp.where(far == 0, 0, main), SUB)
@@ -323,7 +357,7 @@
         def _():
             for index in range(len(hops)):
                 rim_copy(index).wait_recv()
-                arrived(0, 1 + index)
+                arrived(0, index=index)
 
         starts = run_starts(number, strips)
 
@@ -350,9 +384,15 @@
         size = UNROLL * SUB
         lax.fori_loop(0, HALO // size, partly, 0)
 
+        @pl.when(jnp.logical_and(number == 0, leads))
+        def _():
+            pl.semaphore_wait(greeted, len(hops))
+            send_rims()
+
         @pl.when(number == 0)
         def _():
-            arrived(0, 0)
+            for piece in pieces:
+                arrived(0, piece)
 
         lax.fori_loop(HALO // size, rows // size, fully, 0)
         return carry
@@ -376,18 +416,20 @@
 
             lax.fori_loop(0, strips_ref.shape[0], repeat, 0)
 
-    lat_copy(0).wait_send()
+    for piece in pieces:
+        lat_copy(0, piece).wait_send()
     for index in range(len(hops)):
         rim_copy(index).wait_send()
         corner_copy(0, index).wait_send()
 
     @pl.when(far_exists)
     def _():
-        lat_copy(1).wait_send()
-        arrived(1, 0)
+        for piece in pieces:
+            lat_copy(1, piece).wait_send()
+            arrived(1, piece)
         for index in range(len(hops)):
             corner_copy(1, index).wait_send()
-            arrived(1, 1 + index)
+            arrived(1, index=index)
 
 
 def shade_far(rows, cols, *refs):
@@ -505,8 +547,10 @@
             pltpu.VMEM((main, LANES), jnp.float32),
             pltpu.SemaphoreType.REGULAR,
             pltpu.SemaphoreType.DMA((3, strips)),
-            pltpu.SemaphoreType.DMA((2, 1 + hops)),
-            pltpu.SemaphoreType.DMA((2, 1 + hops)),
+            pltpu.SemaphoreType.DMA((2, 2)),
+            pltpu.SemaphoreType.DMA((2, 2)),
+            pltpu.SemaphoreType.DMA((2, hops)),
+            pltpu.SemaphoreType.DMA((2, hops)),
             pltpu.SemaphoreType.DMA((hops,)),
             pltpu.SemaphoreType.DMA((hops,)),
         ],

time: 21.7 us -> 21 us (0.968)
  the two profiles are of different devices: /device:TPU:9 before, /device:TPU:13 now
where the time goes in v3:
time: 21 us; the launch traced here: 20.7 us
  Pallas kernels  20.1 us (96%)
  between operations  0.64 us (3%)
    pallas_call x1, Pallas kernels, local(): pl.pallas_call(functools.partial(gather, rows, cols), out_shape=(pltpu.VM...  16.6 us
    pallas_call x1, Pallas kernels, local(): pl.pallas_call(functools.partial(shade_far, rows, cols), out_shape=(jax.S...  3.46 us

profile of v3, /device:TPU:13, one launch (start us, length us, event | category | flops | bytes accessed | tf_op | source)
XLA Modules:
  0.0 20.7 jit_solution(1155042891893924184)
XLA Ops:
  0.6 16.6 %shard_map.38 = (f32[17,392,128]{2,1,0:T(8,128)S(1)}, f32[2,16,64,128]{3,2,1,0:T(8,128)S(1)}, f32[192,2048]{1,0:T(8,128)S(1)}, f32[2,192,2048]{2,1,0:T(8,128)S(1)}, f32[192,2048]{1,0:T(8,128)S(1)}) custom-call(f32[256,2048]{1,0:T(8,128)} %z_ref.1), custom_call_target="tpu_custom_call" | custom-call | tf_op jit(solution)/shard_map/pallas_call | solution.py:530
  17.3 3.5 %shard_map.39 = (f32[256,2048]{1,0:T(8,128)}, f32[2,256,2048]{2,1,0:T(8,128)}, f32[256,2048]{1,0:T(8,128)}) custom-call(f32[17,392,128]{2,1,0:T(8,128)S(1)} %get-tuple-element.8.refs_0_, f32[2,16,64,128]{3,2,1,0:T(8,128)S(1)} %get-tuple-element.9.refs_1_, f32[192,2048]{1,0:T(8,128)S(1)} %get-tuple-element.10.refs_2_, ...), custom_call_target="tpu_custom_call" | custom-call | tf_op jit(solution)/shard_map/pallas_call | solution.py:562

commit v4 on v3

--- a/solution.py
+++ b/solution.py
@@ -174,6 +174,7 @@
 def gather(rows, cols, z_ref, strips_ref, part, slope, facing, shade, *scratch):
     lags, (
         rim,
+        far_rim,
         coef,
         greeted,
         load_sem,
@@ -250,8 +251,7 @@
             pl.semaphore_signal(greeted, inc=1, device_id=(lat, hop), device_id_type=MESH)
 
 
-    quarter = strips // 4
-    pieces = ((1, quarter), (1 + quarter, strips - quarter))
+    pieces = ((1, 1), (strips, 1), (2, strips - 2))
 
     def lat_copy(distant, piece):
         side, other = (far, far_lat) if distant else (near, near_lat)
@@ -267,11 +267,14 @@
         )
 
     def corner_copy(distant, index):
-        side, other = (far, far_lat) if distant else (near, near_lat)
         hop, target = hops[index]
+        source, row, other = (
+            (far_rim, halo(far), lat) if distant else (rim, halo(far), near_lat)
+        )
+        source = source if distant else source.at[pl.ds(edge(near), HALO), :]
         return pltpu.make_async_remote_copy(
-            src_ref=rim.at[pl.ds(edge(side), HALO), :],
-            dst_ref=strips_ref.at[target, pl.ds(halo(1 - side), HALO), :],
+            src_ref=source,
+            dst_ref=strips_ref.at[target, pl.ds(row, HALO), :],
             send_sem=send_sem.at[distant, index],
             recv_sem=recv_sem.at[distant, index],
             device_id=(other, hop),
@@ -308,7 +311,8 @@
 
     @pl.when(far_exists)
     def _():
-        lat_copy(1, pieces[0]).start()
+        for piece in pieces:
+            lat_copy(1, piece).start()
 
     for load in loads_of(1):
         load.wait()
@@ -338,16 +342,8 @@
             rim_copy(index).start()
             corner_copy(0, index).start()
 
-        @pl.when(far_exists)
-        def _():
-            for index in range(len(hops)):
-                corner_copy(1, index).start()
-
     pl.when(follows)(send_rims)
 
-    @pl.when(far_exists)
-    def _():
-        lat_copy(1, pieces[1]).start()
 
     window = Window(strips_ref, rows, strips, far, coef, slope, facing, shade)
     far_base = pl.multiple_of(jnp.where(far == 0, 0, main), SUB)
@@ -394,7 +390,31 @@
             for piece in pieces:
                 arrived(0, piece)
 
-        lax.fori_loop(HALO // size, rows // size, fully, 0)
+        def segment(index, carry):
+            outer = jnp.logical_and(number == 1, far_exists)
+
+            @pl.when(jnp.logical_and(outer, index == 0))
+            def _():
+                for piece in pieces[:2]:
+                    arrived(1, piece)
+                for start in range(0, HALO, SUB):
+                    here = pl.ds(pl.multiple_of(halo(far) + start, SUB), SUB)
+                    far_rim[pl.ds(start, SUB), :] = jnp.where(
+                        lane < HALO, strips_ref[1, here, :], strips_ref[strips, here, :]
+                    )
+
+            @pl.when(jnp.logical_and(outer, index == 1))
+            def _():
+                for hop in range(len(hops)):
+                    corner_copy(1, hop).start()
+
+            first = HALO // size
+            low = jnp.where(index == 0, first, first + 1)
+            high = jnp.where(index == 0, first + 1, rows // size)
+            lax.fori_loop(low, high, fully, 0)
+            return carry
+
+        lax.fori_loop(0, 2, segment, 0)
         return carry
 
     lax.fori_loop(0, 2, half, 0)
@@ -426,7 +446,7 @@
     def _():
         for piece in pieces:
             lat_copy(1, piece).wait_send()
-            arrived(1, piece)
+        arrived(1, pieces[2])
         for index in range(len(hops)):
             corner_copy(1, index).wait_send()
             arrived(1, index=index)
@@ -544,11 +564,12 @@
         ]
         + [
             pltpu.VMEM((rows, LANES), jnp.float32),
+            pltpu.VMEM((HALO, LANES), jnp.float32),
             pltpu.VMEM((main, LANES), jnp.float32),
             pltpu.SemaphoreType.REGULAR,
             pltpu.SemaphoreType.DMA((3, strips)),
-            pltpu.SemaphoreType.DMA((2, 2)),
-            pltpu.SemaphoreType.DMA((2, 2)),
+            pltpu.SemaphoreType.DMA((2, 3)),
+            pltpu.SemaphoreType.DMA((2, 3)),
             pltpu.SemaphoreType.DMA((2, hops)),
             pltpu.SemaphoreType.DMA((2, hops)),
             pltpu.SemaphoreType.DMA((hops,)),

time: 21 us -> 20.3 us (0.967)
  Pallas kernels: 20.1 us -> 19.4 us
    pallas_call x1, Pallas kernels: 16.6 us -> 16 us  [local(): pl.pallas_call(functools.partial(gather, rows, cols), out_shape=(pltpu.VM...]
where the time goes in v4:
time: 20.3 us; the launch traced here: 20.1 us
  Pallas kernels  19.4 us (96%)
  between operations  0.64 us (3%)
    pallas_call x1, Pallas kernels, local(): pl.pallas_call(functools.partial(gather, rows, cols), out_shape=(pltpu.VM...  16 us
    pallas_call x1, Pallas kernels, local(): pl.pallas_call(functools.partial(shade_far, rows, cols), out_shape=(jax.S...  3.46 us

profile of v4, /device:TPU:13, one launch (start us, length us, event | category | flops | bytes accessed | tf_op | source)
XLA Modules:
  0.0 20.1 jit_solution(7691505504723731942)
XLA Ops:
  0.6 16.0 %shard_map.38 = (f32[17,392,128]{2,1,0:T(8,128)S(1)}, f32[2,16,64,128]{3,2,1,0:T(8,128)S(1)}, f32[192,2048]{1,0:T(8,128)S(1)}, f32[2,192,2048]{2,1,0:T(8,128)S(1)}, f32[192,2048]{1,0:T(8,128)S(1)}) custom-call(f32[256,2048]{1,0:T(8,128)} %z_ref.1), custom_call_target="tpu_custom_call" | custom-call | tf_op jit(solution)/shard_map/pallas_call | solution.py:550
  16.6 3.5 %shard_map.39 = (f32[256,2048]{1,0:T(8,128)}, f32[2,256,2048]{2,1,0:T(8,128)}, f32[256,2048]{1,0:T(8,128)}) custom-call(f32[17,392,128]{2,1,0:T(8,128)S(1)} %get-tuple-element.8.refs_0_, f32[2,16,64,128]{3,2,1,0:T(8,128)S(1)} %get-tuple-element.9.refs_1_, f32[192,2048]{1,0:T(8,128)S(1)} %get-tuple-element.10.refs_2_, ...), custom_call_target="tpu_custom_call" | custom-call | tf_op jit(solution)/shard_map/pallas_call | solution.py:583

commit v5 on v4

--- a/solution.py
+++ b/solution.py
@@ -56,12 +56,17 @@
 
 
 def fill_coef(coef_ref, count, first_row, total_rows, total_cols):
-    for start in range(0, count, SUB):
-        position = first_row + start + lax.broadcasted_iota(jnp.int32, (SUB, LANES), 0)
-        spacing = jnp.sin((position.astype(jnp.float32) + 0.5) * (math.pi / total_rows)) * (
-            2.0 * total_rows / total_cols
-        )
-        coef_ref[pl.ds(start, SUB), :] = 1.0 / (8.0 * SCALES * spacing)
+    row = lax.broadcasted_iota(jnp.int32, (SUB, LANES), 0)
+    tile = jnp.minimum(lax.broadcasted_iota(jnp.int32, (SUB, LANES), 1), count // SUB - 1)
+    position = first_row + row + tile * SUB
+    spacing = jnp.sin((position.astype(jnp.float32) + 0.5) * (math.pi / total_rows)) * (
+        2.0 * total_rows / total_cols
+    )
+    coef = 1.0 / (8.0 * SCALES * spacing)
+    for number in range(count // SUB):
+        coef_ref[pl.ds(number * SUB, SUB), :] = jnp.broadcast_to(
+            coef[:, number : number + 1], (SUB, LANES)
+        )
 
 
 class Window:
@@ -232,9 +237,6 @@
 
     main = rows - HALO
     base = pl.multiple_of(jnp.where(far == 0, HALO, 0), SUB)
-    fill_coef(coef, main, lat * rows + base, rows * n_lat, cols * n_lon)
-    for load in loads_of(0):
-        load.wait()
     odd = lax.rem(lon, 2)
     leads = odd == 0
     follows = odd == 1
@@ -257,9 +259,15 @@
         side, other = (far, far_lat) if distant else (near, near_lat)
         part_ = pl.ds(*piece)
         index = pieces.index(piece)
+        source = strips_ref.at[part_, pl.ds(HALO + edge(side), HALO), :]
+        target = strips_ref.at[part_, pl.ds(halo(1 - side), HALO), :]
+        if distant and piece[1] == 1:
+            columns = pl.ds((piece[0] - 1) * LANES, LANES)
+            source = z_ref.at[pl.ds(edge(side), HALO), columns]
+            target = strips_ref.at[piece[0], pl.ds(halo(1 - side), HALO), :]
         return pltpu.make_async_remote_copy(
-            src_ref=strips_ref.at[part_, pl.ds(HALO + edge(side), HALO), :],
-            dst_ref=strips_ref.at[part_, pl.ds(halo(1 - side), HALO), :],
+            src_ref=source,
+            dst_ref=target,
             send_sem=lat_send.at[distant, index],
             recv_sem=lat_recv.at[distant, index],
             device_id=(other, lon),
@@ -281,13 +289,15 @@
             device_id_type=MESH,
         )
 
-    def rim_copy(index):
+    def rim_copy(index, side):
         hop, target = hops[index]
+        middle = rows // 2
+        start = jnp.where((far if side == 0 else near) == 0, 0, middle)
         return pltpu.make_async_remote_copy(
-            src_ref=rim,
-            dst_ref=strips_ref.at[target, pl.ds(HALO, rows), :],
-            send_sem=rim_send.at[index],
-            recv_sem=rim_recv.at[index],
+            src_ref=rim.at[pl.ds(pl.multiple_of(start, SUB), middle), :],
+            dst_ref=strips_ref.at[target, pl.ds(pl.multiple_of(HALO + start, SUB), middle), :],
+            send_sem=rim_send.at[index, side],
+            recv_sem=rim_recv.at[index, side],
             device_id=(lat, hop),
             device_id_type=MESH,
         )
@@ -311,8 +321,16 @@
 
     @pl.when(far_exists)
     def _():
-        for piece in pieces:
+        for piece in pieces[:2]:
             lat_copy(1, piece).start()
+
+    fill_coef(coef, main, lat * rows + base, rows * n_lat, cols * n_lon)
+    for load in loads_of(0):
+        load.wait()
+
+    @pl.when(far_exists)
+    def _():
+        lat_copy(1, pieces[2]).start()
 
     for load in loads_of(1):
         load.wait()
@@ -339,7 +357,8 @@
 
     def send_rims():
         for index in range(len(hops)):
-            rim_copy(index).start()
+            for side in range(2):
+                rim_copy(index, side).start()
             corner_copy(0, index).start()
 
     pl.when(follows)(send_rims)
@@ -352,8 +371,7 @@
         @pl.when(number == 1)
         def _():
             for index in range(len(hops)):
-                rim_copy(index).wait_recv()
-                arrived(0, index=index)
+                rim_copy(index, 0).wait_recv()
 
         starts = run_starts(number, strips)
 
@@ -385,10 +403,11 @@
             pl.semaphore_wait(greeted, len(hops))
             send_rims()
 
-        @pl.when(number == 0)
+        @pl.when(number == 1)
         def _():
-            for piece in pieces:
-                arrived(0, piece)
+            for index in range(len(hops)):
+                rim_copy(index, 1).wait_recv()
+                arrived(0, index=index)
 
         def segment(index, carry):
             outer = jnp.logical_and(number == 1, far_exists)
@@ -408,13 +427,18 @@
                 for hop in range(len(hops)):
                     corner_copy(1, hop).start()
 
-            first = HALO // size
-            low = jnp.where(index == 0, first, first + 1)
-            high = jnp.where(index == 0, first + 1, rows // size)
+            @pl.when(jnp.logical_and(number == 0, index == 2))
+            def _():
+                for piece in pieces:
+                    arrived(0, piece)
+
+            first, last, end = HALO // size, (rows - HALO) // size, rows // size
+            low = jnp.where(index == 0, first, jnp.where(index == 1, first + 1, last))
+            high = jnp.where(index == 0, first + 1, jnp.where(index == 1, last, end))
             lax.fori_loop(low, high, fully, 0)
             return carry
 
-        lax.fori_loop(0, 2, segment, 0)
+        lax.fori_loop(0, 3, segment, 0)
         return carry
 
     lax.fori_loop(0, 2, half, 0)
@@ -439,7 +463,8 @@
     for piece in pieces:
         lat_copy(0, piece).wait_send()
     for index in range(len(hops)):
-        rim_copy(index).wait_send()
+        for side in range(2):
+            rim_copy(index, side).wait_send()
         corner_copy(0, index).wait_send()
 
     @pl.when(far_exists)
@@ -572,8 +597,8 @@
             pltpu.SemaphoreType.DMA((2, 3)),
             pltpu.SemaphoreType.DMA((2, hops)),
             pltpu.SemaphoreType.DMA((2, hops)),
-            pltpu.SemaphoreType.DMA((hops,)),
-            pltpu.SemaphoreType.DMA((hops,)),
+            pltpu.SemaphoreType.DMA((hops, 2)),
+            pltpu.SemaphoreType.DMA((hops, 2)),
         ],
         compiler_params=pltpu.CompilerParams(
             collective_id=0, has_side_effects=True, vmem_limit_bytes=52 * 2**20

time: 20.3 us -> 20.1 us (level)
  the two profiles are of different devices: /device:TPU:13 before, /device:TPU:1 now
where the time goes in v5:
time: 20.1 us; the launch traced here: 19.9 us
  Pallas kernels  19.3 us (96%)
  between operations  0.64 us (3%)
    pallas_call x1, Pallas kernels, local(): pl.pallas_call(functools.partial(gather, rows, cols), out_shape=(pltpu.VM...  15.8 us
    pallas_call x1, Pallas kernels, local(): pl.pallas_call(functools.partial(shade_far, rows, cols), out_shape=(jax.S...  3.46 us

profile of v5, /device:TPU:1, one launch (start us, length us, event | category | flops | bytes accessed | tf_op | source)
XLA Modules:
  0.0 19.9 jit_solution(10168450502924477724)
XLA Ops:
  0.6 15.8 %shard_map.38 = (f32[17,392,128]{2,1,0:T(8,128)S(1)}, f32[2,16,64,128]{3,2,1,0:T(8,128)S(1)}, f32[192,2048]{1,0:T(8,128)S(1)}, f32[2,192,2048]{2,1,0:T(8,128)S(1)}, f32[192,2048]{1,0:T(8,128)S(1)}) custom-call(f32[256,2048]{1,0:T(8,128)} %z_ref.1), custom_call_target="tpu_custom_call" | custom-call | tf_op jit(solution)/shard_map/pallas_call | solution.py:575
  16.5 3.5 %shard_map.39 = (f32[256,2048]{1,0:T(8,128)}, f32[2,256,2048]{2,1,0:T(8,128)}, f32[256,2048]{1,0:T(8,128)}) custom-call(f32[17,392,128]{2,1,0:T(8,128)S(1)} %get-tuple-element.8.refs_0_, f32[2,16,64,128]{3,2,1,0:T(8,128)S(1)} %get-tuple-element.9.refs_1_, f32[192,2048]{1,0:T(8,128)S(1)} %get-tuple-element.10.refs_2_, ...), custom_call_target="tpu_custom_call" | custom-call | tf_op jit(solution)/shard_map/pallas_call | solution.py:608

commit v6 on v5

--- a/solution.py
+++ b/solution.py
@@ -495,8 +495,7 @@
             (
                 (slope, slope_out.at[pl.ds(base, main), :]),
                 (shade, shade_out.at[pl.ds(base, main), :]),
-                (facing.at[0], facing_out.at[0, pl.ds(base, main), :]),
-                (facing.at[1], facing_out.at[1, pl.ds(base, main), :]),
+                (facing, facing_out.at[:, pl.ds(base, main), :]),
             )
         )
     ]
@@ -515,8 +514,7 @@
                 (
                     (slope_far.at[:, column], slope_out.at[here, column]),
                     (shade_far_.at[:, column], shade_out.at[here, column]),
-                    (facing_far.at[0, :, column], facing_out.at[0, here, column]),
-                    (facing_far.at[1, :, column], facing_out.at[1, here, column]),
+                    (facing_far.at[:, :, column], facing_out.at[:, here, column]),
                 )
             ):
                 found.append(
@@ -619,8 +617,8 @@
                 pltpu.VMEM((HALO, cols), jnp.float32),
                 pltpu.VMEM((2, HALO, cols), jnp.float32),
                 pltpu.VMEM((HALO, cols), jnp.float32),
-                pltpu.SemaphoreType.DMA((4,)),
-                pltpu.SemaphoreType.DMA((2, RUNS, 4)),
+                pltpu.SemaphoreType.DMA((3,)),
+                pltpu.SemaphoreType.DMA((2, RUNS, 3)),
             ],
             compiler_params=pltpu.CompilerParams(vmem_limit_bytes=16 * 2**20),
         )(*staged)

time: 20.1 us -> 20.1 us (level)
  no operation moved by 1% of the time
where the time goes in v6:
time: 20.1 us; the launch traced here: 19.9 us
  Pallas kernels  19.3 us (96%)
  between operations  0.64 us (3%)
    pallas_call x1, Pallas kernels, local(): pl.pallas_call(functools.partial(gather, rows, cols), out_shape=(pltpu.VM...  15.8 us
    pallas_call x1, Pallas kernels, local(): pl.pallas_call(functools.partial(shade_far, rows, cols), out_shape=(jax.S...  3.47 us

profile of v6, /device:TPU:1, one launch (start us, length us, event | category | flops | bytes accessed | tf_op | source)
XLA Modules:
  0.0 19.9 jit_solution(7368726403252983622)
XLA Ops:
  0.6 15.8 %shard_map.38 = (f32[17,392,128]{2,1,0:T(8,128)S(1)}, f32[2,16,64,128]{3,2,1,0:T(8,128)S(1)}, f32[192,2048]{1,0:T(8,128)S(1)}, f32[2,192,2048]{2,1,0:T(8,128)S(1)}, f32[192,2048]{1,0:T(8,128)S(1)}) custom-call(f32[256,2048]{1,0:T(8,128)} %z_ref.1), custom_call_target="tpu_custom_call" | custom-call | tf_op jit(solution)/shard_map/pallas_call | solution.py:573
  16.5 3.5 %shard_map.39 = (f32[256,2048]{1,0:T(8,128)}, f32[2,256,2048]{2,1,0:T(8,128)}, f32[256,2048]{1,0:T(8,128)}) custom-call(f32[17,392,128]{2,1,0:T(8,128)S(1)} %get-tuple-element.8.refs_0_, f32[2,16,64,128]{3,2,1,0:T(8,128)S(1)} %get-tuple-element.9.refs_1_, f32[192,2048]{1,0:T(8,128)S(1)} %get-tuple-element.10.refs_2_, ...), custom_call_target="tpu_custom_call" | custom-call | tf_op jit(solution)/shard_map/pallas_call | solution.py:606
